TPU v7x, 512 devices: a whole 4x4x16 slice. The times are simulated.
512 devices in a mesh: wide: 64 (over z, y), narrow: 8 (over x, core).
Axes of the slice: x: 4, y: 4, z: 16, core: 2. Of those that a mesh axis runs over, the one named last changes fastest.
Arguments:
- query_coords: float32 [3, 512, 16, 512], P(None, ('wide', 'narrow')), may hold values from -1 to 1
- owner_element: int32 [512, 16, 512], P(('wide', 'narrow')), may hold values from 0 to 15
- pair_counts: int32 [512, 512], P(('wide', 'narrow')), may hold values from 0 to 16, as said below
- fields: bfloat16 [8192, 8, 1024], P(('wide', 'narrow')), may hold values from -6 to 6
Outputs:
- values: bfloat16 [16, 512, 16, 512], P(None, ('wide', 'narrow'))
Inputs may be any that keep to these rules, and one draw needn't show every extreme that they name: `pair_counts`: every count is at most 16, and some pair of devices reaches 16 in every draw.
All inputs are finite; a program needn't handle non-finite values.
Results may differ from a plain program's by a relative error of at most 0.0043.
Values may be sent and summed in bfloat16 or wider, within the bound.
A program may use at most 64 MiB of HBM per device.

v0:
```python
import math

import jax
import jax.numpy as jnp
from jax import lax
from jax.sharding import PartitionSpec as P

GLL_NODES = (
    -1.0,
    -0.8717401485096066,
    -0.5917001814331423,
    -0.2092992179024789,
    0.2092992179024789,
    0.5917001814331423,
    0.8717401485096066,
    1.0,
)


def for_sending(shard):
    return jax.tree.map(lambda a: a.astype(jnp.bfloat16) if a.dtype == jnp.float32 else a, shard)


def split_up(shard, dim, devices):
    shape = shard.shape
    parts = shard.reshape(*shape[:dim], devices, shape[dim] // devices, *shape[dim + 1 :])
    return jnp.moveaxis(parts, dim, 0)


def laid_out(parts, dim):
    shape = list(parts.shape[1:])
    shape[dim] *= parts.shape[0]
    return jnp.moveaxis(parts, 0, dim).reshape(shape)


def exchange_both(shard, axis, axes, splits, concats):
    sizes = [lax.axis_size(a) for a in axes]
    parts = split_up(shard, splits[0], sizes[0])
    parts = jnp.moveaxis(split_up(parts, splits[1] + 1, sizes[1]), 0, 1)
    inside = parts.shape[2:]
    parts = parts.reshape(-1, *inside)
    parts = lax.all_to_all(parts, axis, split_axis=0, concat_axis=0, tiled=True)
    parts = laid_out(parts.reshape(*sizes, *inside), concats[0] + 1)
    return laid_out(parts, concats[1])


def lagrange(position):
    result = []
    for i in range(8):
        factor = jnp.ones_like(position)
        for m in range(8):
            if m != i:
                factor = factor * ((position - GLL_NODES[m]) / (GLL_NODES[i] - GLL_NODES[m]))
        result.append(factor)
    return jnp.stack(result)


def interpolate(payload, field_table):
    element_count = field_table.shape[0] // 8
    column_count = field_table.shape[1]
    half_cols = column_count // 2
    basis_r = lagrange(payload[0]).astype(jnp.bfloat16)
    tensor_st = (lagrange(payload[1])[:, None, :] * lagrange(payload[2])[None, :, :]).reshape(
        64, -1
    )
    picked = payload[3][None, :] == jnp.arange(element_count, dtype=jnp.float32)[:, None]
    weights = jnp.where(
        picked[:, None, :], basis_r[None, :, :], jnp.zeros((), jnp.bfloat16)
    ).reshape(element_count * 8, -1)
    halves = []
    for h in range(2):
        partial_value = lax.dot_general(
            field_table[:, h * half_cols : (h + 1) * half_cols],
            weights,
            (((0,), (0,)), ((), ())),
            preferred_element_type=jnp.float32,
        )
        halves.append(
            jnp.sum(partial_value.reshape(half_cols // 64, 64, -1) * tensor_st[None, :, :], axis=1)
        )
    return jnp.concatenate(halves, axis=0).astype(jnp.bfloat16)


def evaluate(payload, field_table):
    field_count = field_table.shape[1] // 64
    lead_shape = payload.shape[1:]
    flat = payload.reshape(4, -1)
    total_rows = flat.shape[1]
    block_rows = math.gcd(total_rows, 512)
    blocks = jnp.transpose(flat.reshape(4, total_rows // block_rows, block_rows), (1, 0, 2))

    def one_block(block):
        return interpolate(block, field_table)

    results = lax.map(one_block, blocks)
    return jnp.transpose(results, (1, 0, 2)).reshape((field_count,) + lead_shape)


def on_device(query_coords, owner_element, pair_counts, fields):
    wide_size = lax.axis_size("wide")
    narrow_size = lax.axis_size("narrow")
    device_count = wide_size * narrow_size
    slot_count = owner_element.shape[1]
    element_count = fields.shape[0]
    field_table = fields.reshape(element_count * fields.shape[1], fields.shape[2])
    live = jnp.arange(slot_count, dtype=jnp.int32)[:, None] < pair_counts[0][None, :]
    element_float = jnp.where(live, owner_element[0], element_count).astype(jnp.float32)
    payload = jnp.concatenate([query_coords[:, 0], element_float[None]], axis=0)
    payload = payload.reshape(4, slot_count, wide_size, narrow_size)
    arrived = lax.all_to_all(
        lax.all_to_all(payload, "wide", split_axis=2, concat_axis=2, tiled=True),
        "narrow",
        split_axis=3,
        concat_axis=3,
        tiled=True,
    )
    result = evaluate(arrived, field_table)
    returned = exchange_both(
        for_sending(result), ("wide", "narrow"), ("wide", "narrow"), (2, 3), (2, 3)
    ).astype(result.dtype)
    return returned.reshape(returned.shape[0], 1, slot_count, device_count)


def solution(mesh):
    placed = (
        P(None, ("wide", "narrow"), None, None),
        P(("wide", "narrow"), None, None),
        P(("wide", "narrow"), None),
        P(("wide", "narrow"), None, None),
    )
    return jax.shard_map(
        on_device,
        mesh=mesh,
        in_specs=placed,
        out_specs=P(None, ("wide", "narrow"), None, None),
        check_vma=False,
    )
```

profile of v0, /device:TPU:1, one launch (start us, length us, event | category | flops | bytes accessed | tf_op | source)
XLA Modules:
  0.0 120.6 jit_solution(5787073060896474956)
XLA Ops:
  0.0 0.8 select_convert_fusion
  0.9 1.2 copy.28
  2.2 0.4 reshape.2237
  2.6 34.1 %all_to_all.15 = f32[64,1,512]{2,1,0:T(1,128)S(1)} all-to-all(f32[64,1,512]{2,1,0:T(1,128)S(1)} %reshape.2237), channel_id=1, replica_groups=mesh['wide'=64,'narrow'=8] {'wide'}, dimensions={0} | all-to-all | bytes 262144 | tf_op jit(solution)/shard_map/all_to_all | solution.py:111
  36.7 0.5 broadcast.4025
  37.2 0.9 reduce
  38.1 0.4 reshape.2238
  38.4 0.6 copy.31
  39.1 0.8 reshape.2239
  39.9 7.9 %all-to-all-start.1 = ((f32[8,1,4096]{2,1,0:T(1,128)}), f32[8,1,4096]{2,1,0:T(1,128)S(1)}, u32[]{:S(2)}, u32[]{:S(2)}) async-start(f32[8,1,4096]{2,1,0:T(1,128)} %reshape.2239), calls=%async_computation.1 | async-start | bytes 262144 | tf_op jit(solution)/shard_map/all_to_all | solution.py:110
  47.8 5.2 %all-to-all-done.1 = f32[8,1,4096]{2,1,0:T(1,128)S(1)} async-done(((f32[8,1,4096]{2,1,0:T(1,128)}), f32[8,1,4096]{2,1,0:T(1,128)S(1)}, u32[]{:S(2)}, u32[]{:S(2)}) %all-to-all-start.1) | async-done | bytes 131104 | tf_op jit(solution)/shard_map/all_to_all | solution.py:110
  53.0 0.9 reduce.1
  54.0 0.4 copy.32
  54.7 18.2 %while.13 = (s32[]{:T(128)}, bf16[16,16,512]{2,1,0:T(8,128)(2,1)S(1)}, f32[16,4,512]{2,1,0:T(4,128)S(1)}, bf16[128,1024]{1,0:T(8,128)(2,1)S(1)}, s32[]{:T(128)}, /*index=5*/s32[]{:T(128)}, s32[]{}, s32[]{}, s32[]{}) while((s32[]{:T(128)}, bf16[16,16,512]{2,1,0:T(8,128)(2,1)S(1)}, f32[16,4,512]{2,1,0:T(4,128)S(1)}, ...), condition=%wide.region_3.4_spmd, body=%wide.region_0.3_spmd.sunk | while | flops 135646208 | bytes 2887837 | solution.py:95
  55.2 0.3 fusion.21
  55.5 0.4 multiply_reduce_fusion.3
  56.3 0.3 fusion.21
  56.6 0.4 multiply_reduce_fusion.3
  57.4 0.3 fusion.21
  57.8 0.4 multiply_reduce_fusion.3
  58.9 0.4 multiply_reduce_fusion.3
  59.7 0.3 fusion.21
  60.1 0.4 multiply_reduce_fusion.3
  60.9 0.3 fusion.21
  61.2 0.4 multiply_reduce_fusion.3
  62.3 0.4 multiply_reduce_fusion.3
  63.1 0.3 fusion.21
  63.5 0.4 multiply_reduce_fusion.3
  64.3 0.3 fusion.21
  64.6 0.4 multiply_reduce_fusion.3
  65.8 0.4 multiply_reduce_fusion.3
  66.6 0.3 fusion.21
  66.9 0.4 multiply_reduce_fusion.3
  67.7 0.3 fusion.21
  68.0 0.4 multiply_reduce_fusion.3
  69.2 0.4 multiply_reduce_fusion.3
  70.0 0.3 fusion.21
  70.3 0.4 multiply_reduce_fusion.3
  71.1 0.3 fusion.21
  71.5 0.4 multiply_reduce_fusion.3
  72.6 0.4 multiply_reduce_fusion.3
  73.0 1.0 copy.34
  74.0 2.7 %copy.45 = bf16[512,16,16,1,1]{2,1,4,3,0:T(8,128)(2,1)} copy(bf16[512,16,16,1,1]{2,0,1,4,3:T(8,128)(2,1)S(1)} %bitcast.127) | data formatting | bytes 524288 | tf_op jit(solution)/shard_map/reshape | solution.py:41
  76.7 3.4 %reshape.2241 = bf16[512,2,128]{2,1,0:T(2,128)(2,1)S(1)} reshape(bf16[512,1,1,16,16]{4,3,2,1,0:T(8,128)(2,1)} %bitcast.128) | data formatting | bytes 524288
  80.1 34.3 %all_to_all.16 = bf16[512,2,128]{2,1,0:T(2,128)(2,1)S(1)} all-to-all(bf16[512,2,128]{2,1,0:T(2,128)(2,1)S(1)} %reshape.2241), channel_id=1, replica_groups=mesh['wide'=64,'narrow'=8] {'wide','narrow'}, dimensions={0} | all-to-all | bytes 524288 | tf_op jit(solution)/shard_map/all_to_all | solution.py:42
  114.4 1.3 %reshape.2242 = bf16[512,1,1,16,16]{4,3,2,1,0:T(8,128)(2,1)S(1)} reshape(bf16[512,2,128]{2,1,0:T(2,128)(2,1)S(1)} %all_to_all.16) | data formatting | bytes 524288
  115.7 1.7 %bitcast_bitcast_fusion = bf16[16,1,16,512]{2,0,3,1:T(8,128)(2,1)} fusion(bf16[512,1,1,16,16]{4,3,2,1,0:T(8,128)(2,1)S(1)} %reshape.2242), kind=kLoop, calls=%fused_computation.78 | loop fusion | bytes 524288 | tf_op jit(solution)/shard_map/reshape;reshape | solution.py:121
  117.4 3.1 %copy.38 = bf16[16,1,16,512]{3,2,1,0:T(8,128)(2,1)} copy(bf16[16,1,16,512]{2,0,3,1:T(8,128)(2,1)} %bitcast_bitcast_fusion) | data formatting | bytes 524288 | tf_op jit(solution)/shard_map/reshape;reshape | solution.py:121
  (140 shorter events, 8.4 us)
Async XLA Ops:
  39.1 15.7 %copy-start = (bf16[16,8,1024]{2,1,0:T(8,128)(2,1)S(1)}, bf16[16,8,1024]{2,1,0:T(8,128)(2,1)}, u32[]{:S(2)}) copy-start(bf16[16,8,1024]{2,1,0:T(8,128)(2,1)} %param.9) | copy-start | bytes 786436
  39.9 13.1 %all-to-all-start.1 = ((f32[8,1,4096]{2,1,0:T(1,128)}), f32[8,1,4096]{2,1,0:T(1,128)S(1)}, u32[]{:S(2)}, u32[]{:S(2)}) async-start(f32[8,1,4096]{2,1,0:T(1,128)} %reshape.2239), calls=%async_computation.1 | async-start | bytes 262144 | tf_op jit(solution)/shard_map/all_to_all | solution.py:110
where the time goes:
time: 121 us
  blocking collectives  68.4 us (57%)
  local copies, waits for them, and re-layouts  20.1 us (17%)
  matrix products  11.1 us (9%)
  starting transfers between devices  7.88 us (7%)
  other arithmetic  6.76 us (6%)
  waiting for transfers between devices  5.24 us (4%)
    all_to_all x1, blocking collectives, exchange_both(): parts = lax.all_to_all(parts, axis, split_axis=0, concat_axis=0, tiled=True)  34.3 us
    all_to_all x1, blocking collectives, on_device(): lax.all_to_all(payload, 'wide', split_axis=2, concat_axis=2, tiled=True)  34.1 us
    dot_general x32, matrix products, interpolate(): lax.dot_general(field_table[:, h * half_cols:(h + 1) * half_cols], weight...  11.1 us
    all_to_all x1, starting transfers between devices, on_device(): lax.all_to_all(lax.all_to_all(payload, 'wide', split_axis=2, concat_axis=...  7.88 us
    unnamed x9, local copies, waits for them, and re-layouts  7.56 us
    all_to_all x1, waiting for transfers between devices, on_device(): lax.all_to_all(lax.all_to_all(payload, 'wide', split_axis=2, concat_axis=...  5.24 us
    another operation x2, local copies, waits for them, and re-layouts, on_device(): return returned.reshape(returned.shape[0], 1, slot_count, device_count)  4.84 us
    reshape x1, local copies, waits for them, and re-layouts, exchange_both(): parts = parts.reshape(-1, *inside)  2.7 us
  transfers between devices with their start and end apart: 1, of which 1 were waited for; matrix products, arithmetic and copies ran while one was open for 0% of the time, Pallas kernels for 0%

commit v1 on v0

v1 whole, which is shorter than its diff:
```python
import functools

import jax
import jax.numpy as jnp
from jax import lax
from jax.experimental import pallas as pl
from jax.experimental.pallas import tpu as pltpu
from jax.sharding import PartitionSpec as P

GLL_NODES = (
    -1.0,
    -0.8717401485096066,
    -0.5917001814331423,
    -0.2092992179024789,
    0.2092992179024789,
    0.5917001814331423,
    0.8717401485096066,
    1.0,
)
MESH = pl.DeviceIdType.MESH
NZ = 16
NQ = 32
NY = 4
NX = 8


def node_constants():
    rows = []
    scale = []
    for i in range(8):
        product = 1.0
        for m in range(8):
            if m != i:
                product *= GLL_NODES[i] - GLL_NODES[m]
        scale.append(1.0 / product)
    rows.append(scale)
    for k in range(1, 8):
        rows.append([GLL_NODES[(i + k) % 8] for i in range(8)])
    return rows


def sublane_constant(values):
    index = lax.broadcasted_iota(jnp.int32, (8, 128), 0)
    result = jnp.full((8, 128), values[0], jnp.float32)
    for i in range(1, 8):
        result = jnp.where(index == i, jnp.float32(values[i]), result)
    return result


def lagrange(position, consts):
    result = consts[0]
    for k in range(1, 8):
        result = result * (position - consts[k])
    return result


def encode(x):
    return (x * 32767.0 + 32768.5).astype(jnp.int32)


def decode(u):
    return (u - 32768).astype(jnp.float32) * jnp.float32(1.0 / 32767.0)


def kernel(
    qc, oe, pc, fl, out,
    ft, gf, ee, sq, rq, sz, rz, ts, vs, rv, srf, sr, rr, orf,
    qs_sem, qr_sem, zs_sem, zr_sem, vs_sem, vr_sem, ws_sem, wr_sem,
):
    wide = lax.axis_index("wide")
    narrow = lax.axis_index("narrow")
    z = wide // NY
    y = wide % NY
    q = y * NX + narrow

    def plane_peer(k):
        peer = (q + k) % NQ
        return peer, (z * NY + peer // NX, peer % NX)

    def z_peer(k):
        peer = (z + k) % NZ
        return peer, (peer * NY + y, narrow)

    barrier = pltpu.get_barrier_semaphore()

    def greet_plane(k, carry):
        pl.semaphore_signal(barrier, inc=1, device_id=plane_peer(k)[1], device_id_type=MESH)
        return carry

    def greet_z(k, carry):
        pl.semaphore_signal(barrier, inc=1, device_id=z_peer(k)[1], device_id_type=MESH)
        return carry

    lax.fori_loop(1, NZ, greet_z, 0)
    lax.fori_loop(1, NQ, greet_plane, 0)

    for h in range(4):
        rows = pl.ds(4 * h, 4)
        slot = lax.broadcasted_iota(jnp.int32, (4, 512), 0) + 4 * h
        live = slot < pc[0:1, :]
        element = jnp.where(live, oe[0, rows, :], 16)
        ee[h, 0:4, :] = jnp.left_shift(encode(qc[0, 0, rows, :]), 16) + encode(qc[1, 0, rows, :])
        ee[h, 4:8, :] = jnp.left_shift(encode(qc[2, 0, rows, :]), 16) + element
    group = lax.broadcasted_iota(jnp.int32, (8, 128), 1) // 32
    blocks = []
    for t in range(4):
        pieces = [ee[h, :, t * 128 : (t + 1) * 128] for h in range(4)]
        for zl in range(4):
            block = None
            for h in range(4):
                shift = ((h - zl) * 32) % 128
                piece = pieces[h] if shift == 0 else pltpu.roll(pieces[h], shift, 1)
                block = piece if block is None else jnp.where(group == h, piece, block)
            blocks.append(block)
    turned = jnp.transpose(jnp.concatenate(blocks, axis=0))
    for h in range(4):
        sq[:, h, :] = turned[h * 32 : (h + 1) * 32, :]

    for b in range(8):
        part = fl[:, :, b * 128 : (b + 1) * 128].reshape(128, 128).astype(jnp.float32)
        gf[b * 128 : (b + 1) * 128, :] = jnp.transpose(part)

    def permute(n, carry):
        ft[pl.ds(pl.multiple_of(n * 16, 16), 16), :] = gf[pl.ds(n, 16, stride=64), :].astype(jnp.bfloat16)
        return carry

    lax.fori_loop(0, 64, permute, 0)
    consts = [sublane_constant(v) for v in node_constants()]

    pl.semaphore_wait(barrier, NQ - 1 + NZ - 1)

    def plane_copy(src, dst, send, recv, k):
        peer, device = plane_peer(k)
        return pltpu.make_async_remote_copy(
            src_ref=src.at[peer], dst_ref=dst.at[q], send_sem=send.at[peer], recv_sem=recv.at[q],
            device_id=device, device_id_type=MESH,
        )

    def plane_arrival(src, dst, send, recv, k):
        peer, device = plane_peer(k)
        return pltpu.make_async_remote_copy(
            src_ref=src.at[peer], dst_ref=dst.at[peer], send_sem=send.at[peer], recv_sem=recv.at[peer],
            device_id=device, device_id_type=MESH,
        )

    def z_copy(src, dst, send, recv, k):
        peer, device = z_peer(k)
        return pltpu.make_async_remote_copy(
            src_ref=src.at[peer], dst_ref=dst.at[z], send_sem=send.at[peer], recv_sem=recv.at[z],
            device_id=device, device_id_type=MESH,
        )

    def z_arrival(src, dst, send, recv, k):
        peer, device = z_peer(k)
        return pltpu.make_async_remote_copy(
            src_ref=src.at[peer], dst_ref=dst.at[peer], send_sem=send.at[peer], recv_sem=recv.at[peer],
            device_id=device, device_id_type=MESH,
        )

    def each(low, high, do):
        def step(k, carry):
            do(k)
            return carry

        lax.fori_loop(low, high, step, 0)

    each(1, NQ, lambda k: plane_copy(sq, rq, qs_sem, qr_sem, k).start())
    rq[pl.ds(q, 1)] = sq[pl.ds(q, 1)]
    each(1, NQ, lambda k: plane_arrival(sq, rq, qs_sem, qr_sem, k).wait_recv())
    gathered = jnp.concatenate([rq[:, h, :] for h in range(4)], axis=0)
    sz[...] = jnp.transpose(gathered).reshape(NZ, 8, 128)

    def far_first(k):
        n = NZ - k
        return ((n + 1) // 2 * (2 * (n % 2) - 1) + NZ) % NZ

    def near_first(k):
        return ((k + 1) // 2 * (2 * (k % 2) - 1) + NZ) % NZ

    each(1, NZ, lambda k: z_copy(sz, rz, zs_sem, zr_sem, far_first(k)).start())
    rz[pl.ds(z, 1)] = sz[pl.ds(z, 1)]

    def evaluate(peer):
        weights = []
        for sl in range(4):
            lanes = slice(sl * 128, (sl + 1) * 128)
            w0 = jnp.broadcast_to(rz[peer, sl : sl + 1, :], (8, 128))
            w1 = jnp.broadcast_to(rz[peer, 4 + sl : 5 + sl, :], (8, 128))
            basis_r = lagrange(decode(lax.shift_right_logical(w0, 16)), consts)
            basis_s = lagrange(decode(jnp.bitwise_and(w0, 65535)), consts)
            basis_t = lagrange(decode(lax.shift_right_logical(w1, 16)), consts)
            element = jnp.bitwise_and(w1, 65535)
            weights.append(
                jnp.concatenate(
                    [jnp.where(element == e, basis_r, 0.0) for e in range(16)], axis=0
                ).astype(jnp.bfloat16)
            )
            for j in range(8):
                ts[j * 8 : (j + 1) * 8, lanes] = basis_s[j : j + 1, :] * basis_t
        for half in range(2):
            pair = jnp.concatenate(weights[2 * half : 2 * half + 2], axis=1)
            lanes = slice(half * 256, (half + 1) * 256)
            partial = jnp.dot(ft[...], pair, preferred_element_type=jnp.float32)
            total = None
            for n in range(64):
                term = partial[n * 16 : (n + 1) * 16, :] * ts[n : n + 1, lanes]
                total = term if total is None else total + term
            rounded = total.astype(jnp.bfloat16)
            vs[peer, 2 * half] = rounded[:, :128]
            vs[peer, 2 * half + 1] = rounded[:, 128:]

    evaluate(z)
    rv[pl.ds(z, 1)] = vs[pl.ds(z, 1)]

    def remote_step(k, carry):
        offset = near_first(k)
        z_arrival(sz, rz, zs_sem, zr_sem, offset).wait_recv()
        evaluate((z + offset) % NZ)
        z_copy(vs, rv, vs_sem, vr_sem, offset).start()
        return carry

    lax.fori_loop(1, NZ, remote_step, 0)
    each(1, NZ, lambda k: z_arrival(vs, rv, vs_sem, vr_sem, near_first(k)).wait_recv())

    def turn_back(g, carry):
        zl = g // 2
        first = (g % 2) * 8 + zl
        both = jnp.concatenate(
            [rv[first].reshape(64, 128), rv[first + 4].reshape(64, 128)], axis=0
        ).astype(jnp.float32)
        rows = jnp.transpose(both)
        for h in range(4):
            srf[pl.ds(g * 4 + h, 32, stride=32), :] = rows[h * 32 : (h + 1) * 32, :]
        return carry

    lax.fori_loop(0, 8, turn_back, 0)

    def narrow_down(n, carry):
        sr[n] = srf[pl.ds(pl.multiple_of(n * 32, 32), 32), :].astype(jnp.bfloat16)
        return carry

    lax.fori_loop(0, NQ, narrow_down, 0)
    each(1, NQ, lambda k: plane_copy(sr, rr, ws_sem, wr_sem, k).start())
    rr[pl.ds(q, 1)] = sr[pl.ds(q, 1)]
    each(1, NQ, lambda k: plane_arrival(sr, rr, ws_sem, wr_sem, k).wait_recv())

    def widen(n, carry):
        srf[pl.ds(pl.multiple_of(n * 32, 32), 32), :] = rr[n].astype(jnp.float32)
        return carry

    lax.fori_loop(0, NQ, widen, 0)
    for t_hi in range(2):
        for h in range(4):
            rows = jnp.concatenate(
                [srf[pl.ds((zl * 2 + t_hi) * 4 + h, 32, stride=32), :] for zl in range(4)], axis=0
            )
            turned = jnp.transpose(rows)
            for t_lo in range(2):
                for sl in range(4):
                    at = t_lo * 64 + sl * 16
                    orf[2 * t_hi + t_lo, pl.ds(h * 4 + sl, 16, stride=16), :] = turned[at : at + 16, :]
    for t in range(4):
        for c in range(16):
            out[c, 0, :, t * 128 : (t + 1) * 128] = orf[t, c * 16 : (c + 1) * 16, :].astype(jnp.bfloat16)

    each(1, NQ, lambda k: plane_copy(sq, rq, qs_sem, qr_sem, k).wait_send())
    each(1, NZ, lambda k: z_copy(sz, rz, zs_sem, zr_sem, k).wait_send())
    each(1, NZ, lambda k: z_copy(vs, rv, vs_sem, vr_sem, k).wait_send())
    each(1, NQ, lambda k: plane_copy(sr, rr, ws_sem, wr_sem, k).wait_send())


def on_device(query_coords, owner_element, pair_counts, fields):
    vmem = pl.BlockSpec(memory_space=pltpu.VMEM)
    return pl.pallas_call(
        kernel,
        out_shape=jax.ShapeDtypeStruct((16, 1, 16, 512), jnp.bfloat16),
        in_specs=[vmem] * 4,
        out_specs=vmem,
        scratch_shapes=[
            pltpu.VMEM((1024, 128), jnp.bfloat16),
            pltpu.VMEM((1024, 128), jnp.float32),
            pltpu.VMEM((4, 8, 512), jnp.int32),
            pltpu.VMEM((NQ, 4, 128), jnp.int32),
            pltpu.VMEM((NQ, 4, 128), jnp.int32),
            pltpu.VMEM((NZ, 8, 128), jnp.int32),
            pltpu.VMEM((NZ, 8, 128), jnp.int32),
            pltpu.VMEM((64, 512), jnp.float32),
            pltpu.VMEM((NZ, 4, 16, 128), jnp.bfloat16),
            pltpu.VMEM((NZ, 4, 16, 128), jnp.bfloat16),
            pltpu.VMEM((NQ * 32, 128), jnp.float32),
            pltpu.VMEM((NQ, 32, 128), jnp.bfloat16),
            pltpu.VMEM((NQ, 32, 128), jnp.bfloat16),
            pltpu.VMEM((4, 256, 128), jnp.float32),
            pltpu.SemaphoreType.DMA((NQ,)),
            pltpu.SemaphoreType.DMA((NQ,)),
            pltpu.SemaphoreType.DMA((NZ,)),
            pltpu.SemaphoreType.DMA((NZ,)),
            pltpu.SemaphoreType.DMA((NZ,)),
            pltpu.SemaphoreType.DMA((NZ,)),
            pltpu.SemaphoreType.DMA((NQ,)),
            pltpu.SemaphoreType.DMA((NQ,)),
        ],
        compiler_params=pltpu.CompilerParams(collective_id=0, has_side_effects=True),
    )(query_coords, owner_element, pair_counts, fields)


def solution(mesh):
    placed = (
        P(None, ("wide", "narrow"), None, None),
        P(("wide", "narrow"), None, None),
        P(("wide", "narrow"), None),
        P(("wide", "narrow"), None, None),
    )
    return jax.shard_map(
        on_device,
        mesh=mesh,
        in_specs=placed,
        out_specs=P(None, ("wide", "narrow"), None, None),
        check_vma=False,
    )
```

time: 121 us -> 56.7 us (0.47)
  blocking collectives: 68.4 us -> 0 us
  Pallas kernels: 0 us -> 54.8 us
  local copies, waits for them, and re-layouts: 20.1 us -> 1.67 us
  matrix products: 11.1 us -> 0 us
  starting transfers between devices: 7.88 us -> 0 us
  other arithmetic: 6.76 us -> 0 us
  waiting for transfers between devices: 5.24 us -> 0 us
    all_to_all x2 -> x0, blocking collectives: 68.4 us -> none  [the longest x1 34.3 us: exchange_both(): parts = lax.all_to_all(parts, axis, split_axis=0, concat_axis=0, tiled=True)]
    pallas_call x0 -> x1, Pallas kernels: none -> 54.8 us  [on_device(): pl.pallas_call(kernel, out_shape=jax.ShapeDtypeStruct((16, 1, 16, 512), j...]
    dot_general x32 -> x0, matrix products: 11.1 us -> none  [interpolate(): lax.dot_general(field_table[:, h * half_cols:(h + 1) * half_cols], weight...]
    all_to_all x1 -> x0, starting transfers between devices: 7.88 us -> none  [on_device(): lax.all_to_all(lax.all_to_all(payload, 'wide', split_axis=2, concat_axis=...]
    another operation x50 -> x0, local copies, waits for them, and re-layouts: 6.79 us -> none  [the longest x2 4.84 us: on_device(): return returned.reshape(returned.shape[0], 1, slot_count, device_count)]
    unnamed x9 -> x1, local copies, waits for them, and re-layouts: 7.56 us -> 1.67 us
    all_to_all x1 -> x0, waiting for transfers between devices: 5.24 us -> none  [on_device(): lax.all_to_all(lax.all_to_all(payload, 'wide', split_axis=2, concat_axis=...]
    reshape x1 -> x0, local copies, waits for them, and re-layouts: 2.7 us -> none  [exchange_both(): parts = parts.reshape(-1, *inside)]
  transfers between devices with their start and end apart: 1 -> 0, of which waited for: 1 -> 0; matrix products, arithmetic and copies ran while one was open for 0% -> 0% of each run, Pallas kernels for 0% -> 0%
where the time goes in v1:
time: 56.7 us; the launch traced here: 56.5 us
  Pallas kernels  54.8 us (97%)
  local copies, waits for them, and re-layouts  1.67 us (3%)
    pallas_call x1, Pallas kernels, on_device(): pl.pallas_call(kernel, out_shape=jax.ShapeDtypeStruct((16, 1, 16, 512), j...  54.8 us
    unnamed x1, local copies, waits for them, and re-layouts  1.67 us

profile of v1, /device:TPU:1, one launch (start us, length us, event | category | flops | bytes accessed | tf_op | source)
XLA Modules:
  0.0 56.5 jit_solution(10343876748625749087)
XLA Ops:
  0.0 54.8 %shard_map.46 = bf16[16,1,16,512]{3,2,1,0:T(8,128)(2,1)} custom-call(f32[3,1,16,512]{3,2,1,0:T(8,128)} %qc.1, s32[1,16,512]{2,1,0:T(8,128)} %oe.1, s32[1,512]{1,0:T(1,128)} %pc.1, bf16[16,8,1024]{2,1,0:T(8,128)(2,1)} %fl.1), custom_call_target="tpu_custom_call" | custom-call | tf_op jit(solution)/shard_map/pallas_call | solution.py:274
  54.8 1.7 %copy.6 = bf16[16,1,16,512]{3,2,1,0:T(8,128)(2,1)} copy(bf16[16,1,16,512]{3,2,1,0:T(8,128)(2,1)} %shard_map.46) | data formatting | bytes 524288

commit v2 on v1

v2 whole, which is shorter than its diff:
```python
import functools

import jax
import jax.numpy as jnp
from jax import lax
from jax.experimental import pallas as pl
from jax.experimental.pallas import tpu as pltpu
from jax.sharding import PartitionSpec as P

GLL_NODES = (
    -1.0,
    -0.8717401485096066,
    -0.5917001814331423,
    -0.2092992179024789,
    0.2092992179024789,
    0.5917001814331423,
    0.8717401485096066,
    1.0,
)
MESH = pl.DeviceIdType.MESH
NZ = 16
NQ = 32
NY = 4
NX = 8
NEAR = 10
GROUPS = 4


def node_constants():
    rows = []
    scale = []
    for i in range(8):
        product = 1.0
        for m in range(8):
            if m != i:
                product *= GLL_NODES[i] - GLL_NODES[m]
        scale.append(1.0 / product)
    rows.append(scale)
    for k in range(1, 8):
        rows.append([GLL_NODES[(i + k) % 8] for i in range(8)])
    return rows


def sublane_constant(values):
    index = lax.broadcasted_iota(jnp.int32, (8, 128), 0)
    result = jnp.full((8, 128), values[0], jnp.float32)
    for i in range(1, 8):
        result = jnp.where(index == i, jnp.float32(values[i]), result)
    return result


def lagrange(position, consts):
    result = consts[0]
    for k in range(1, 8):
        result = result * (position - consts[k])
    return result


def encode(x):
    return (x * 32767.0 + 32768.5).astype(jnp.int32)


def decode(u):
    return (u - 32768).astype(jnp.float32) * jnp.float32(1.0 / 32767.0)


def position_to_nearness(k):
    late = lax.div(k + 15 - NEAR, 16)
    return k * (1 - late) + (NZ + NEAR - k) * late


def nearness_to_offset(n):
    return lax.rem(lax.div(n + 1, 2) * (2 * lax.rem(n, 2) - 1) + NZ, NZ)


def offset_to_position(o):
    side = lax.div(o + 7, 16)
    n = (2 * o - lax.div(o + 15, 16)) * (1 - side) + (2 * NZ - 2 * o) * side
    return position_to_nearness(n)


def each(low, high, do):
    def step(k, carry):
        do(k)
        return carry

    lax.fori_loop(low, high, step, 0)


def kernel(
    qc_hbm, oe_hbm, pc_hbm, fl_hbm, rr,
    qc, oe, pc, fl, ft, gf, ee, sq, rq, sz, rz, ts, vs, rv, srf, sr,
    in_sem, qs_sem, qr_sem, zs_sem, zr_sem, vs_sem, vr_sem, ws_sem, wr_sem, own_sem,
):
    wide = lax.axis_index("wide")
    narrow = lax.axis_index("narrow")
    z = lax.div(wide, NY)
    y = lax.rem(wide, NY)
    q = y * NX + narrow

    def plane_peer(k):
        peer = lax.rem(q + k, NQ)
        return peer, (z * NY + lax.div(peer, NX), lax.rem(peer, NX))

    def z_peer(o):
        peer = lax.rem(z + o, NZ)
        return peer, (peer * NY + y, narrow)

    loads = [
        pltpu.make_async_copy(src, dst, in_sem.at[n])
        for n, (src, dst) in enumerate(((qc_hbm, qc), (oe_hbm, oe), (pc_hbm, pc), (fl_hbm, fl)))
    ]
    barrier = pltpu.get_barrier_semaphore()

    def greet_plane(k):
        pl.semaphore_signal(barrier, inc=1, device_id=plane_peer(k)[1], device_id_type=MESH)

    def greet_z(k):
        device = z_peer(nearness_to_offset(NZ - k))[1]
        pl.semaphore_signal(barrier, inc=1, device_id=device, device_id_type=MESH)

    with jax.named_scope("greet"):
        for load in loads:
            load.start()
        each(1, NZ, greet_z)
        each(1, NQ, greet_plane)

    with jax.named_scope("load"):
        for load in loads[:3]:
            load.wait()

    with jax.named_scope("encode"):
        for h in range(4):
            rows = pl.ds(4 * h, 4)
            slot = lax.broadcasted_iota(jnp.int32, (4, 512), 0) + 4 * h
            live = slot < pc[0:1, :]
            element = jnp.where(live, oe[0, rows, :], 16)
            ee[h, 0:4, :] = jnp.left_shift(encode(qc[0, 0, rows, :]), 16) + encode(qc[1, 0, rows, :])
            ee[h, 4:8, :] = jnp.left_shift(encode(qc[2, 0, rows, :]), 16) + element
        group = lax.broadcasted_iota(jnp.int32, (8, 128), 1) // 32
        blocks = []
        for t in range(4):
            pieces = [ee[h, :, t * 128 : (t + 1) * 128] for h in range(4)]
            for zl in range(4):
                block = None
                for h in range(4):
                    shift = ((h - zl) * 32) % 128
                    piece = pieces[h] if shift == 0 else pltpu.roll(pieces[h], shift, 1)
                    block = piece if block is None else jnp.where(group == h, piece, block)
                blocks.append(block)
        turned = jnp.transpose(jnp.concatenate(blocks, axis=0))
        for h in range(4):
            sq[:, h, :] = turned[h * 32 : (h + 1) * 32, :]

    with jax.named_scope("barrier"):
        pl.semaphore_wait(barrier, NQ - 1 + NZ - 1)

    def plane_copy(src, dst, send, recv, k):
        peer, device = plane_peer(k)
        return pltpu.make_async_remote_copy(
            src_ref=src.at[peer], dst_ref=dst.at[q], send_sem=send, recv_sem=recv,
            device_id=device, device_id_type=MESH,
        )

    def plane_all(src, dst, send, recv):
        others = pl.ds(0, NQ - 1)
        return pltpu.make_async_remote_copy(
            src_ref=src.at[others], dst_ref=dst.at[others], send_sem=send, recv_sem=recv,
            device_id=plane_peer(1)[1], device_id_type=MESH,
        )

    def z_copy(src, dst, send, recv, o):
        peer, device = z_peer(o)
        return pltpu.make_async_remote_copy(
            src_ref=src.at[peer], dst_ref=dst.at[z], send_sem=send, recv_sem=recv.at[z],
            device_id=device, device_id_type=MESH,
        )

    def z_arrival(src, dst, send, recv, o):
        peer, device = z_peer(o)
        return pltpu.make_async_remote_copy(
            src_ref=src.at[peer], dst_ref=dst.at[peer], send_sem=send, recv_sem=recv.at[peer],
            device_id=device, device_id_type=MESH,
        )

    def z_all(src, dst, send, recv):
        others = pl.ds(0, NZ - 1)
        return pltpu.make_async_remote_copy(
            src_ref=src.at[others], dst_ref=dst.at[others], send_sem=send, recv_sem=recv.at[0],
            device_id=z_peer(1)[1], device_id_type=MESH,
        )

    with jax.named_scope("plane_send"):
        each(1, NQ, lambda k: plane_copy(sq, rq, qs_sem.at[0], qr_sem.at[0], k).start())
        rq[pl.ds(q, 1)] = sq[pl.ds(q, 1)]

    def permute(n):
        ft[pl.ds(pl.multiple_of(n * 16, 16), 16), :] = gf[pl.ds(n, 16, stride=64), :].astype(jnp.bfloat16)

    with jax.named_scope("table"):
        loads[3].wait()
        for b in range(8):
            part = fl[:, :, b * 128 : (b + 1) * 128].reshape(128, 128).astype(jnp.float32)
            gf[b * 128 : (b + 1) * 128, :] = jnp.transpose(part)
        each(0, 64, permute)
    consts = [sublane_constant(v) for v in node_constants()]

    with jax.named_scope("plane_wait"):
        plane_all(sq, rq, qs_sem.at[0], qr_sem.at[0]).wait_recv()
    with jax.named_scope("turn_queries"):
        gathered = jnp.concatenate([rq[:, h, :] for h in range(4)], axis=0)
        sz[...] = jnp.transpose(gathered).reshape(NZ, 8, 128)

    with jax.named_scope("z_send"):
        each(1, NZ, lambda k: z_copy(sz, rz, zs_sem.at[0], zr_sem, nearness_to_offset(k)).start())
        rz[pl.ds(z, 1)] = sz[pl.ds(z, 1)]

    def evaluate(peer):
        weights = []
        for sl in range(4):
            lanes = slice(sl * 128, (sl + 1) * 128)
            w0 = jnp.broadcast_to(rz[peer, sl : sl + 1, :], (8, 128))
            w1 = jnp.broadcast_to(rz[peer, 4 + sl : 5 + sl, :], (8, 128))
            basis_r = lagrange(decode(lax.shift_right_logical(w0, 16)), consts)
            basis_s = lagrange(decode(jnp.bitwise_and(w0, 65535)), consts)
            basis_t = lagrange(decode(lax.shift_right_logical(w1, 16)), consts)
            element = jnp.bitwise_and(w1, 65535)
            weights.append(
                jnp.concatenate(
                    [jnp.where(element == e, basis_r, 0.0) for e in range(16)], axis=0
                ).astype(jnp.bfloat16)
            )
            for j in range(8):
                ts[j * 8 : (j + 1) * 8, lanes] = basis_s[j : j + 1, :] * basis_t
        for half in range(2):
            pair = jnp.concatenate(weights[2 * half : 2 * half + 2], axis=1)
            lanes = slice(half * 256, (half + 1) * 256)
            partial = jnp.dot(ft[...], pair, preferred_element_type=jnp.float32)
            total = None
            for n in range(64):
                term = partial[n * 16 : (n + 1) * 16, :] * ts[n : n + 1, lanes]
                total = term if total is None else total + term
            rounded = total.astype(jnp.bfloat16)
            vs[peer, 2 * half] = rounded[:, :128]
            vs[peer, 2 * half + 1] = rounded[:, 128:]

    with jax.named_scope("own"):
        evaluate(z)
        rv[pl.ds(z, 1)] = vs[pl.ds(z, 1)]

    def remote_step(k):
        offset = nearness_to_offset(position_to_nearness(k))
        with jax.named_scope("z_wait"):
            z_arrival(sz, rz, zs_sem.at[0], zr_sem, offset).wait_recv()
        with jax.named_scope("evaluate"):
            evaluate(lax.rem(z + offset, NZ))
            z_copy(vs, rv, vs_sem.at[0], vr_sem, offset).start()

    each(1, NZ, remote_step)

    def turn_back(n, at):
        offset = nearness_to_offset(position_to_nearness(n))
        block = rv[lax.rem(z + offset, NZ)].reshape(64, 128).astype(jnp.float32)
        rows = jnp.transpose(jnp.concatenate([block, pltpu.roll(block, 96, 1)], axis=0))
        for half in range(2):
            srf[pl.ds(2 * at + half, 32, stride=8), :] = rows[half * 64 : half * 64 + 32, :]

    def return_group(g, first):
        def wait(n):
            offset = nearness_to_offset(position_to_nearness(n))
            z_arrival(vs, rv, vs_sem.at[0], vr_sem, offset).wait_recv()

        with jax.named_scope("z_return"):
            each(first, 4 * g + 4, wait)
        with jax.named_scope("turn_back"):
            for at in range(4):
                turn_back(4 * g + at, at)
            sr[g] = srf[...].reshape(NQ, 8, 128).astype(jnp.bfloat16)
        with jax.named_scope("plane_return"):
            each(1, NQ, lambda k: plane_copy(sr.at[g], rr.at[g], ws_sem.at[g], wr_sem.at[g], k).start())
            pltpu.make_async_copy(sr.at[g, q], rr.at[g, q], own_sem.at[g]).start()

    for g in range(GROUPS):
        return_group(g, max(4 * g, 1))
    with jax.named_scope("drain"):
        plane_all(sq, rq, qs_sem.at[0], qr_sem.at[0]).wait_send()
        z_all(sz, rz, zs_sem.at[0], zr_sem).wait_send()
        z_all(vs, rv, vs_sem.at[0], vr_sem).wait_send()
    with jax.named_scope("plane_back"):
        for g in range(GROUPS):
            plane_all(sr.at[g], rr.at[g], ws_sem.at[g], wr_sem.at[g]).wait_recv()
            pltpu.make_async_copy(sr.at[g, q], rr.at[g, q], own_sem.at[g]).wait()
    with jax.named_scope("drain2"):
        for g in range(GROUPS):
            plane_all(sr.at[g], rr.at[g], ws_sem.at[g], wr_sem.at[g]).wait_send()


def finish(rr_hbm, out_hbm, rr, srf, orf, staged, sem, in_sem):
    loads = [pltpu.make_async_copy(rr_hbm.at[g], rr.at[g], in_sem.at[g]) for g in range(GROUPS)]
    for load in loads:
        load.start()
    z = lax.div(lax.axis_index("wide"), NY)

    with jax.named_scope("widen"):
        for g in range(GROUPS):
            loads[g].wait()
            srf[g] = rr[g].reshape(NQ * 8, 128).astype(jnp.float32)
    copies = []
    for t in range(4):
        with jax.named_scope("finish"):
            for half in range(2):
                parts = []
                for zl in range(4):
                    position = offset_to_position(lax.rem(t * 4 + zl - z + NZ, NZ))
                    row = lax.rem(position, 4) * 2 + half
                    parts.append(srf[lax.div(position, 4), pl.ds(row, 32, stride=8), :])
                turned = jnp.transpose(jnp.concatenate(parts, axis=0))
                for n in range(8):
                    orf[t, pl.ds(half * 8 + n, 16, stride=16), :] = turned[n * 16 : (n + 1) * 16, :]
            staged[t] = orf[t].reshape(16, 16, 128).astype(jnp.bfloat16)
            copy = pltpu.make_async_copy(
                staged.at[t], out_hbm.at[:, 0, :, pl.ds(t * 128, 128)], sem.at[t]
            )
            copy.start()
            copies.append(copy)
    with jax.named_scope("store"):
        for copy in copies:
            copy.wait()


def on_device(query_coords, owner_element, pair_counts, fields):
    anywhere = pl.BlockSpec(memory_space=pl.ANY)
    vmem = pl.BlockSpec(memory_space=pltpu.VMEM)
    returned = pl.pallas_call(
        kernel,
        out_shape=jax.ShapeDtypeStruct((GROUPS, NQ, 8, 128), jnp.bfloat16),
        in_specs=[anywhere] * 4,
        out_specs=anywhere,
        scratch_shapes=[
            pltpu.VMEM((3, 1, 16, 512), jnp.float32),
            pltpu.VMEM((1, 16, 512), jnp.int32),
            pltpu.VMEM((1, 512), jnp.int32),
            pltpu.VMEM((16, 8, 1024), jnp.bfloat16),
            pltpu.VMEM((1024, 128), jnp.bfloat16),
            pltpu.VMEM((1024, 128), jnp.float32),
            pltpu.VMEM((4, 8, 512), jnp.int32),
            pltpu.VMEM((NQ, 4, 128), jnp.int32),
            pltpu.VMEM((NQ, 4, 128), jnp.int32),
            pltpu.VMEM((NZ, 8, 128), jnp.int32),
            pltpu.VMEM((NZ, 8, 128), jnp.int32),
            pltpu.VMEM((64, 512), jnp.float32),
            pltpu.VMEM((NZ, 4, 16, 128), jnp.bfloat16),
            pltpu.VMEM((NZ, 4, 16, 128), jnp.bfloat16),
            pltpu.VMEM((NQ * 8, 128), jnp.float32),
            pltpu.VMEM((GROUPS, NQ, 8, 128), jnp.bfloat16),
            pltpu.SemaphoreType.DMA((4,)),
            pltpu.SemaphoreType.DMA((1,)),
            pltpu.SemaphoreType.DMA((1,)),
            pltpu.SemaphoreType.DMA((1,)),
            pltpu.SemaphoreType.DMA((NZ,)),
            pltpu.SemaphoreType.DMA((1,)),
            pltpu.SemaphoreType.DMA((NZ,)),
            pltpu.SemaphoreType.DMA((GROUPS,)),
            pltpu.SemaphoreType.DMA((GROUPS,)),
            pltpu.SemaphoreType.DMA((GROUPS,)),
        ],
        compiler_params=pltpu.CompilerParams(collective_id=0, has_side_effects=True),
    )(query_coords, owner_element, pair_counts, fields)
    return pl.pallas_call(
        finish,
        out_shape=jax.ShapeDtypeStruct((16, 1, 16, 512), jnp.bfloat16),
        in_specs=[anywhere],
        out_specs=anywhere,
        scratch_shapes=[
            pltpu.VMEM((GROUPS, NQ, 8, 128), jnp.bfloat16),
            pltpu.VMEM((GROUPS, NQ * 8, 128), jnp.float32),
            pltpu.VMEM((4, 256, 128), jnp.float32),
            pltpu.VMEM((4, 16, 16, 128), jnp.bfloat16),
            pltpu.SemaphoreType.DMA((4,)),
            pltpu.SemaphoreType.DMA((GROUPS,)),
        ],
    )(returned)


def solution(mesh):
    placed = (
        P(None, ("wide", "narrow"), None, None),
        P(("wide", "narrow"), None, None),
        P(("wide", "narrow"), None),
        P(("wide", "narrow"), None, None),
    )
    return jax.shard_map(
        on_device,
        mesh=mesh,
        in_specs=placed,
        out_specs=P(None, ("wide", "narrow"), None, None),
        check_vma=False,
    )
```

time: 56.7 us -> 49.5 us (0.87)
  Pallas kernels: 54.8 us -> 49.3 us
  local copies, waits for them, and re-layouts: 1.67 us -> 0 us
    pallas_call x1 -> x2, Pallas kernels: 54.8 us -> 49.3 us  [the longest x1 47.2 us: on_device(): pl.pallas_call(kernel, out_shape=jax.ShapeDtypeStruct((GROUPS, NQ, 8, 128...]
    unnamed x1 -> x0, local copies, waits for them, and re-layouts: 1.67 us -> none
where the time goes in v2:
time: 49.5 us; the launch traced here: 49.3 us
  Pallas kernels  49.3 us (100%)
    pallas_call x1, Pallas kernels, on_device(): pl.pallas_call(kernel, out_shape=jax.ShapeDtypeStruct((GROUPS, NQ, 8, 128...  47.2 us
    pallas_call x1, Pallas kernels, on_device(): pl.pallas_call(finish, out_shape=jax.ShapeDtypeStruct((16, 1, 16, 512), j...  2.04 us

profile of v2, /device:TPU:1, one launch (start us, length us, event | category | flops | bytes accessed | tf_op | source)
XLA Modules:
  0.0 49.3 jit_solution(11691933768679789407)
XLA Ops:
  0.0 47.2 %shard_map.46.rr_hbm = bf16[4,32,8,128]{3,2,1,0:T(8,128)(2,1)} custom-call(f32[3,1,16,512]{3,2,1,0:T(8,128)} %qc_hbm.1, s32[1,16,512]{2,1,0:T(8,128)} %oe_hbm.1, s32[1,512]{1,0:T(1,128)} %pc_hbm.1, bf16[16,8,1024]{2,1,0:T(8,128)(2,1)} %fl_hbm.1), custom_call_target="tpu_custom_call" | custom-call | tf_op jit(solution)/shard_map/pallas_call | solution.py:334
  47.2 2.0 %shard_map.47 = bf16[16,1,16,512]{3,2,1,0:T(8,128)(2,1)} custom-call(bf16[4,32,8,128]{3,2,1,0:T(8,128)(2,1)} %shard_map.46.rr_hbm), custom_call_target="tpu_custom_call" | custom-call | tf_op jit(solution)/shard_map/pallas_call | solution.py:369

commit v3 on v2

--- a/solution.py
+++ b/solution.py
@@ -17,7 +17,7 @@
     0.8717401485096066,
     1.0,
 )
-MESH = pl.DeviceIdType.MESH
+LOGICAL = pl.DeviceIdType.LOGICAL
 NZ = 16
 NQ = 32
 NY = 4
@@ -70,10 +70,11 @@
 
 
 def nearness_to_offset(n):
-    return lax.rem(lax.div(n + 1, 2) * (2 * lax.rem(n, 2) - 1) + NZ, NZ)
+    return lax.rem(lax.div(n + 1, 2) * (1 - 2 * lax.rem(n, 2)) + NZ, NZ)
 
 
 def offset_to_position(o):
+    o = lax.rem(NZ - o, NZ)
     side = lax.div(o + 7, 16)
     n = (2 * o - lax.div(o + 15, 16)) * (1 - side) + (2 * NZ - 2 * o) * side
     return position_to_nearness(n)
@@ -90,21 +91,22 @@
 def kernel(
     qc_hbm, oe_hbm, pc_hbm, fl_hbm, rr,
     qc, oe, pc, fl, ft, gf, ee, sq, rq, sz, rz, ts, vs, rv, srf, sr,
-    in_sem, qs_sem, qr_sem, zs_sem, zr_sem, vs_sem, vr_sem, ws_sem, wr_sem, own_sem,
+    in_sem, qs_sem, qr_sem, zs_sem, zr_sem, vs_sem, vr_sem, ws_sem, wr_sem, own_sem, told,
 ):
     wide = lax.axis_index("wide")
     narrow = lax.axis_index("narrow")
     z = lax.div(wide, NY)
-    y = lax.rem(wide, NY)
-    q = y * NX + narrow
+    q = lax.rem(wide, NY) * NX + narrow
+    me = z * NQ + q
+    core = lax.rem(narrow, 2)
 
     def plane_peer(k):
         peer = lax.rem(q + k, NQ)
-        return peer, (z * NY + lax.div(peer, NX), lax.rem(peer, NX))
+        return peer, z * NQ + peer
 
     def z_peer(o):
         peer = lax.rem(z + o, NZ)
-        return peer, (peer * NY + y, narrow)
+        return peer, peer * NQ + q
 
     loads = [
         pltpu.make_async_copy(src, dst, in_sem.at[n])
@@ -113,17 +115,22 @@
     barrier = pltpu.get_barrier_semaphore()
 
     def greet_plane(k):
-        pl.semaphore_signal(barrier, inc=1, device_id=plane_peer(k)[1], device_id_type=MESH)
+        chip = lax.rem(lax.div(q, 2) + k, NQ // 2)
+        pl.semaphore_signal(barrier, inc=1, device_id=z * NQ + 2 * chip, device_id_type=LOGICAL)
 
     def greet_z(k):
-        device = z_peer(nearness_to_offset(NZ - k))[1]
-        pl.semaphore_signal(barrier, inc=1, device_id=device, device_id_type=MESH)
+        peer = z_peer(nearness_to_offset(NZ - k))[1]
+        pl.semaphore_signal(barrier, inc=1, device_id=peer - core + 1, device_id_type=LOGICAL)
 
     with jax.named_scope("greet"):
         for load in loads:
             load.start()
         each(1, NZ, greet_z)
-        each(1, NQ, greet_plane)
+        each(1, NQ // 2, greet_plane)
+
+        @pl.when(core == 1)
+        def _():
+            pl.semaphore_signal(barrier, inc=1, device_id=me - 1, device_id_type=LOGICAL)
 
     with jax.named_scope("load"):
         for load in loads[:3]:
@@ -153,41 +160,49 @@
             sq[:, h, :] = turned[h * 32 : (h + 1) * 32, :]
 
     with jax.named_scope("barrier"):
-        pl.semaphore_wait(barrier, NQ - 1 + NZ - 1)
+
+        @pl.when(core == 0)
+        def _():
+            pl.semaphore_wait(barrier, NQ - 1)
+            pl.semaphore_signal(told, inc=1, device_id=me + 1, device_id_type=LOGICAL)
+
+        @pl.when(core == 1)
+        def _():
+            pl.semaphore_wait(told, 1)
 
     def plane_copy(src, dst, send, recv, k):
         peer, device = plane_peer(k)
         return pltpu.make_async_remote_copy(
             src_ref=src.at[peer], dst_ref=dst.at[q], send_sem=send, recv_sem=recv,
-            device_id=device, device_id_type=MESH,
+            device_id=device, device_id_type=LOGICAL,
         )
 
     def plane_all(src, dst, send, recv):
         others = pl.ds(0, NQ - 1)
         return pltpu.make_async_remote_copy(
             src_ref=src.at[others], dst_ref=dst.at[others], send_sem=send, recv_sem=recv,
-            device_id=plane_peer(1)[1], device_id_type=MESH,
+            device_id=plane_peer(1)[1], device_id_type=LOGICAL,
         )
 
     def z_copy(src, dst, send, recv, o):
         peer, device = z_peer(o)
         return pltpu.make_async_remote_copy(
             src_ref=src.at[peer], dst_ref=dst.at[z], send_sem=send, recv_sem=recv.at[z],
-            device_id=device, device_id_type=MESH,
+            device_id=device, device_id_type=LOGICAL,
         )
 
     def z_arrival(src, dst, send, recv, o):
         peer, device = z_peer(o)
         return pltpu.make_async_remote_copy(
             src_ref=src.at[peer], dst_ref=dst.at[peer], send_sem=send, recv_sem=recv.at[peer],
-            device_id=device, device_id_type=MESH,
+            device_id=device, device_id_type=LOGICAL,
         )
 
     def z_all(src, dst, send, recv):
         others = pl.ds(0, NZ - 1)
         return pltpu.make_async_remote_copy(
             src_ref=src.at[others], dst_ref=dst.at[others], send_sem=send, recv_sem=recv.at[0],
-            device_id=z_peer(1)[1], device_id_type=MESH,
+            device_id=z_peer(1)[1], device_id_type=LOGICAL,
         )
 
     with jax.named_scope("plane_send"):
@@ -204,6 +219,17 @@
             gf[b * 128 : (b + 1) * 128, :] = jnp.transpose(part)
         each(0, 64, permute)
     consts = [sublane_constant(v) for v in node_constants()]
+
+    with jax.named_scope("barrier_z"):
+
+        @pl.when(core == 1)
+        def _():
+            pl.semaphore_wait(barrier, 2 * (NZ - 1))
+            pl.semaphore_signal(told, inc=1, device_id=me - 1, device_id_type=LOGICAL)
+
+        @pl.when(core == 0)
+        def _():
+            pl.semaphore_wait(told, 1)
 
     with jax.named_scope("plane_wait"):
         plane_all(sq, rq, qs_sem.at[0], qr_sem.at[0]).wait_recv()
@@ -363,6 +389,7 @@
             pltpu.SemaphoreType.DMA((GROUPS,)),
             pltpu.SemaphoreType.DMA((GROUPS,)),
             pltpu.SemaphoreType.DMA((GROUPS,)),
+            pltpu.SemaphoreType.REGULAR,
         ],
         compiler_params=pltpu.CompilerParams(collective_id=0, has_side_effects=True),
     )(query_coords, owner_element, pair_counts, fields)

time: 49.5 us -> 48.2 us (0.974)
  Pallas kernels: 49.3 us -> 48 us
    pallas_call x1, Pallas kernels: 47.2 us -> 45.9 us  [on_device(): pl.pallas_call(kernel, out_shape=jax.ShapeDtypeStruct((GROUPS, NQ, 8, 128...]
where the time goes in v3:
time: 48.2 us; the launch traced here: 48 us
  Pallas kernels  48 us (100%)
    pallas_call x1, Pallas kernels, on_device(): pl.pallas_call(kernel, out_shape=jax.ShapeDtypeStruct((GROUPS, NQ, 8, 128...  45.9 us
    pallas_call x1, Pallas kernels, on_device(): pl.pallas_call(finish, out_shape=jax.ShapeDtypeStruct((16, 1, 16, 512), j...  2.05 us

profile of v3, /device:TPU:1, one launch (start us, length us, event | category | flops | bytes accessed | tf_op | source)
XLA Modules:
  0.0 48.0 jit_solution(6001716931783763945)
XLA Ops:
  0.0 45.9 %shard_map.46.rr_hbm = bf16[4,32,8,128]{3,2,1,0:T(8,128)(2,1)} custom-call(f32[3,1,16,512]{3,2,1,0:T(8,128)} %qc_hbm.1, s32[1,16,512]{2,1,0:T(8,128)} %oe_hbm.1, s32[1,512]{1,0:T(1,128)} %pc_hbm.1, bf16[16,8,1024]{2,1,0:T(8,128)(2,1)} %fl_hbm.1), custom_call_target="tpu_custom_call" | custom-call | tf_op jit(solution)/shard_map/pallas_call | solution.py:360
  45.9 2.1 %shard_map.47 = bf16[16,1,16,512]{3,2,1,0:T(8,128)(2,1)} custom-call(bf16[4,32,8,128]{3,2,1,0:T(8,128)(2,1)} %shard_map.46.rr_hbm), custom_call_target="tpu_custom_call" | custom-call | tf_op jit(solution)/shard_map/pallas_call | solution.py:396

commit v4 on v3

--- a/solution.py
+++ b/solution.py
@@ -73,11 +73,7 @@
     return lax.rem(lax.div(n + 1, 2) * (1 - 2 * lax.rem(n, 2)) + NZ, NZ)
 
 
-def offset_to_position(o):
-    o = lax.rem(NZ - o, NZ)
-    side = lax.div(o + 7, 16)
-    n = (2 * o - lax.div(o + 15, 16)) * (1 - side) + (2 * NZ - 2 * o) * side
-    return position_to_nearness(n)
+ORDER = (0, 15, 1, 14, 2, 13, 3, 12, 4, 11, 5, 8, 7, 9, 6, 10)
 
 
 def each(low, high, do):
@@ -119,18 +115,22 @@
         pl.semaphore_signal(barrier, inc=1, device_id=z * NQ + 2 * chip, device_id_type=LOGICAL)
 
     def greet_z(k):
-        peer = z_peer(nearness_to_offset(NZ - k))[1]
+        peer = z_peer(k)[1]
         pl.semaphore_signal(barrier, inc=1, device_id=peer - core + 1, device_id_type=LOGICAL)
 
     with jax.named_scope("greet"):
         for load in loads:
             load.start()
-        each(1, NZ, greet_z)
-        each(1, NQ // 2, greet_plane)
+        for k in range(1, NQ // 2):
+            greet_plane(k)
 
         @pl.when(core == 1)
         def _():
             pl.semaphore_signal(barrier, inc=1, device_id=me - 1, device_id_type=LOGICAL)
+
+        for distance in range(NZ // 2, 0, -1):
+            for offset in sorted({NZ - distance, distance}):
+                greet_z(offset)
 
     with jax.named_scope("load"):
         for load in loads[:3]:
@@ -206,7 +206,8 @@
         )
 
     with jax.named_scope("plane_send"):
-        each(1, NQ, lambda k: plane_copy(sq, rq, qs_sem.at[0], qr_sem.at[0], k).start())
+        for k in range(1, NQ):
+            plane_copy(sq, rq, qs_sem.at[0], qr_sem.at[0], k).start()
         rq[pl.ds(q, 1)] = sq[pl.ds(q, 1)]
 
     def permute(n):
@@ -238,7 +239,9 @@
         sz[...] = jnp.transpose(gathered).reshape(NZ, 8, 128)
 
     with jax.named_scope("z_send"):
-        each(1, NZ, lambda k: z_copy(sz, rz, zs_sem.at[0], zr_sem, nearness_to_offset(k)).start())
+        for distance in range(1, NZ // 2 + 1):
+            for offset in sorted({NZ - distance, distance}, reverse=True):
+                z_copy(sz, rz, zs_sem.at[0], zr_sem, offset).start()
         rz[pl.ds(z, 1)] = sz[pl.ds(z, 1)]
 
     def evaluate(peer):
@@ -285,25 +288,22 @@
     each(1, NZ, remote_step)
 
     def turn_back(n, at):
-        offset = nearness_to_offset(position_to_nearness(n))
-        block = rv[lax.rem(z + offset, NZ)].reshape(64, 128).astype(jnp.float32)
+        block = rv[lax.rem(z + ORDER[n], NZ)].reshape(64, 128).astype(jnp.float32)
         rows = jnp.transpose(jnp.concatenate([block, pltpu.roll(block, 96, 1)], axis=0))
         for half in range(2):
             srf[pl.ds(2 * at + half, 32, stride=8), :] = rows[half * 64 : half * 64 + 32, :]
 
     def return_group(g, first):
-        def wait(n):
-            offset = nearness_to_offset(position_to_nearness(n))
-            z_arrival(vs, rv, vs_sem.at[0], vr_sem, offset).wait_recv()
-
         with jax.named_scope("z_return"):
-            each(first, 4 * g + 4, wait)
+            for n in range(first, 4 * g + 4):
+                z_arrival(vs, rv, vs_sem.at[0], vr_sem, ORDER[n]).wait_recv()
         with jax.named_scope("turn_back"):
             for at in range(4):
                 turn_back(4 * g + at, at)
             sr[g] = srf[...].reshape(NQ, 8, 128).astype(jnp.bfloat16)
         with jax.named_scope("plane_return"):
-            each(1, NQ, lambda k: plane_copy(sr.at[g], rr.at[g], ws_sem.at[g], wr_sem.at[g], k).start())
+            for k in range(1, NQ):
+                plane_copy(sr.at[g], rr.at[g], ws_sem.at[g], wr_sem.at[g], k).start()
             pltpu.make_async_copy(sr.at[g, q], rr.at[g, q], own_sem.at[g]).start()
 
     for g in range(GROUPS):
@@ -321,7 +321,7 @@
             plane_all(sr.at[g], rr.at[g], ws_sem.at[g], wr_sem.at[g]).wait_send()
 
 
-def finish(rr_hbm, out_hbm, rr, srf, orf, staged, sem, in_sem):
+def finish(rr_hbm, out_hbm, rr, srf, rows, orf, staged, sem, in_sem):
     loads = [pltpu.make_async_copy(rr_hbm.at[g], rr.at[g], in_sem.at[g]) for g in range(GROUPS)]
     for load in loads:
         load.start()
@@ -331,16 +331,15 @@
         for g in range(GROUPS):
             loads[g].wait()
             srf[g] = rr[g].reshape(NQ * 8, 128).astype(jnp.float32)
+            for n in range(4):
+                owner = lax.rem(z + ORDER[4 * g + n], NZ)
+                for half in range(2):
+                    rows[owner, half] = srf[g, pl.ds(2 * n + half, NQ, stride=8), :]
     copies = []
     for t in range(4):
         with jax.named_scope("finish"):
             for half in range(2):
-                parts = []
-                for zl in range(4):
-                    position = offset_to_position(lax.rem(t * 4 + zl - z + NZ, NZ))
-                    row = lax.rem(position, 4) * 2 + half
-                    parts.append(srf[lax.div(position, 4), pl.ds(row, 32, stride=8), :])
-                turned = jnp.transpose(jnp.concatenate(parts, axis=0))
+                turned = jnp.transpose(jnp.concatenate([rows[t * 4 + zl, half] for zl in range(4)], axis=0))
                 for n in range(8):
                     orf[t, pl.ds(half * 8 + n, 16, stride=16), :] = turned[n * 16 : (n + 1) * 16, :]
             staged[t] = orf[t].reshape(16, 16, 128).astype(jnp.bfloat16)
@@ -401,6 +400,7 @@
         scratch_shapes=[
             pltpu.VMEM((GROUPS, NQ, 8, 128), jnp.bfloat16),
             pltpu.VMEM((GROUPS, NQ * 8, 128), jnp.float32),
+            pltpu.VMEM((NZ, 2, NQ, 128), jnp.float32),
             pltpu.VMEM((4, 256, 128), jnp.float32),
             pltpu.VMEM((4, 16, 16, 128), jnp.bfloat16),
             pltpu.SemaphoreType.DMA((4,)),

time: 48.2 us -> 47.7 us (0.990)
  Pallas kernels: 48 us -> 47.5 us
where the time goes in v4:
time: 47.7 us; the launch traced here: 47.5 us
  Pallas kernels  47.5 us (100%)
    pallas_call x1, Pallas kernels, on_device(): pl.pallas_call(kernel, out_shape=jax.ShapeDtypeStruct((GROUPS, NQ, 8, 128...  45.6 us
    pallas_call x1, Pallas kernels, on_device(): pl.pallas_call(finish, out_shape=jax.ShapeDtypeStruct((16, 1, 16, 512), j...  1.94 us

profile of v4, /device:TPU:1, one launch (start us, length us, event | category | flops | bytes accessed | tf_op | source)
XLA Modules:
  0.0 47.5 jit_solution(1393957313282839103)
XLA Ops:
  0.0 45.6 %shard_map.46.rr_hbm = bf16[4,32,8,128]{3,2,1,0:T(8,128)(2,1)} custom-call(f32[3,1,16,512]{3,2,1,0:T(8,128)} %qc_hbm.1, s32[1,16,512]{2,1,0:T(8,128)} %oe_hbm.1, s32[1,512]{1,0:T(1,128)} %pc_hbm.1, bf16[16,8,1024]{2,1,0:T(8,128)(2,1)} %fl_hbm.1), custom_call_target="tpu_custom_call" | custom-call | tf_op jit(solution)/shard_map/pallas_call | solution.py:359
  45.6 1.9 %shard_map.47 = bf16[16,1,16,512]{3,2,1,0:T(8,128)(2,1)} custom-call(bf16[4,32,8,128]{3,2,1,0:T(8,128)(2,1)} %shard_map.46.rr_hbm), custom_call_target="tpu_custom_call" | custom-call | tf_op jit(solution)/shard_map/pallas_call | solution.py:395

commit v5 on v4

--- a/solution.py
+++ b/solution.py
@@ -64,9 +64,9 @@
     return (u - 32768).astype(jnp.float32) * jnp.float32(1.0 / 32767.0)
 
 
-def position_to_nearness(k):
-    late = lax.div(k + 15 - NEAR, 16)
-    return k * (1 - late) + (NZ + NEAR - k) * late
+def position_to_nearness(k, near):
+    late = lax.div(k + 15 - near, 16)
+    return k * (1 - late) + (NZ + near - k) * late
 
 
 def nearness_to_offset(n):
@@ -278,7 +278,7 @@
         rv[pl.ds(z, 1)] = vs[pl.ds(z, 1)]
 
     def remote_step(k):
-        offset = nearness_to_offset(position_to_nearness(k))
+        offset = nearness_to_offset(position_to_nearness(k, 10 - 4 * core))
         with jax.named_scope("z_wait"):
             z_arrival(sz, rz, zs_sem.at[0], zr_sem, offset).wait_recv()
         with jax.named_scope("evaluate"):

time: 47.7 us -> 47.6 us (level)
  no operation moved by 1% of the time
where the time goes in v5:
time: 47.6 us; the launch traced here: 47.4 us
  Pallas kernels  47.4 us (100%)
    pallas_call x1, Pallas kernels, on_device(): pl.pallas_call(kernel, out_shape=jax.ShapeDtypeStruct((GROUPS, NQ, 8, 128...  45.5 us
    pallas_call x1, Pallas kernels, on_device(): pl.pallas_call(finish, out_shape=jax.ShapeDtypeStruct((16, 1, 16, 512), j...  1.94 us

profile of v5, /device:TPU:1, one launch (start us, length us, event | category | flops | bytes accessed | tf_op | source)
XLA Modules:
  0.0 47.4 jit_solution(5687239167192078441)
XLA Ops:
  0.0 45.5 %shard_map.46.rr_hbm = bf16[4,32,8,128]{3,2,1,0:T(8,128)(2,1)} custom-call(f32[3,1,16,512]{3,2,1,0:T(8,128)} %qc_hbm.1, s32[1,16,512]{2,1,0:T(8,128)} %oe_hbm.1, s32[1,512]{1,0:T(1,128)} %pc_hbm.1, bf16[16,8,1024]{2,1,0:T(8,128)(2,1)} %fl_hbm.1), custom_call_target="tpu_custom_call" | custom-call | tf_op jit(solution)/shard_map/pallas_call | solution.py:359
  45.5 1.9 %shard_map.47 = bf16[16,1,16,512]{3,2,1,0:T(8,128)(2,1)} custom-call(bf16[4,32,8,128]{3,2,1,0:T(8,128)(2,1)} %shard_map.46.rr_hbm), custom_call_target="tpu_custom_call" | custom-call | tf_op jit(solution)/shard_map/pallas_call | solution.py:395

commit v6 on v5

--- a/solution.py
+++ b/solution.py
@@ -293,13 +293,13 @@
         for half in range(2):
             srf[pl.ds(2 * at + half, 32, stride=8), :] = rows[half * 64 : half * 64 + 32, :]
 
-    def return_group(g, first):
+    def return_group(g):
         with jax.named_scope("z_return"):
-            for n in range(first, 4 * g + 4):
-                z_arrival(vs, rv, vs_sem.at[0], vr_sem, ORDER[n]).wait_recv()
+            for n in range(4 * g, 4 * g + 4):
+                if n > 0:
+                    z_arrival(vs, rv, vs_sem.at[0], vr_sem, ORDER[n]).wait_recv()
+                turn_back(n, n - 4 * g)
         with jax.named_scope("turn_back"):
-            for at in range(4):
-                turn_back(4 * g + at, at)
             sr[g] = srf[...].reshape(NQ, 8, 128).astype(jnp.bfloat16)
         with jax.named_scope("plane_return"):
             for k in range(1, NQ):
@@ -307,7 +307,7 @@
             pltpu.make_async_copy(sr.at[g, q], rr.at[g, q], own_sem.at[g]).start()
 
     for g in range(GROUPS):
-        return_group(g, max(4 * g, 1))
+        return_group(g)
     with jax.named_scope("drain"):
         plane_all(sq, rq, qs_sem.at[0], qr_sem.at[0]).wait_send()
         z_all(sz, rz, zs_sem.at[0], zr_sem).wait_send()

time: 47.6 us -> 47.8 us (level)
  no operation moved by 1% of the time
where the time goes in v6:
time: 47.8 us; the launch traced here: 47.6 us
  Pallas kernels  47.6 us (100%)
    pallas_call x1, Pallas kernels, on_device(): pl.pallas_call(kernel, out_shape=jax.ShapeDtypeStruct((GROUPS, NQ, 8, 128...  45.7 us
    pallas_call x1, Pallas kernels, on_device(): pl.pallas_call(finish, out_shape=jax.ShapeDtypeStruct((16, 1, 16, 512), j...  1.94 us

profile of v6, /device:TPU:1, one launch (start us, length us, event | category | flops | bytes accessed | tf_op | source)
XLA Modules:
  0.0 47.6 jit_solution(13762263302482802938)
XLA Ops:
  0.0 45.7 %shard_map.46.rr_hbm = bf16[4,32,8,128]{3,2,1,0:T(8,128)(2,1)} custom-call(f32[3,1,16,512]{3,2,1,0:T(8,128)} %qc_hbm.1, s32[1,16,512]{2,1,0:T(8,128)} %oe_hbm.1, s32[1,512]{1,0:T(1,128)} %pc_hbm.1, bf16[16,8,1024]{2,1,0:T(8,128)(2,1)} %fl_hbm.1), custom_call_target="tpu_custom_call" | custom-call | tf_op jit(solution)/shard_map/pallas_call | solution.py:359
  45.7 1.9 %shard_map.47 = bf16[16,1,16,512]{3,2,1,0:T(8,128)(2,1)} custom-call(bf16[4,32,8,128]{3,2,1,0:T(8,128)(2,1)} %shard_map.46.rr_hbm), custom_call_target="tpu_custom_call" | custom-call | tf_op jit(solution)/shard_map/pallas_call | solution.py:395
